TPU v7x, 32 devices: a whole 2x2x4 slice. The times are simulated.
32 devices in a mesh: seq: 8 (over y, x, core), mp: 4 (over z).
Axes of the slice: x: 2, y: 2, z: 4, core: 2. Of those that a mesh axis runs over, the one named last changes fastest.
Arguments:
- frames: bfloat16 [192, 250, 256], P('seq'), may hold values from -7.5 to 7.5
- intra_qkv: bfloat16 [256, 3, 256], P(None, None, 'mp'), may hold values from -20 to 20
- intra_out: bfloat16 [256, 256], P('mp'), may hold values from -0.375 to 0.375
- intra_up: bfloat16 [256, 1024], P(None, 'mp'), may hold values from -0.375 to 0.375
- intra_down: bfloat16 [1024, 256], P('mp'), may hold values from -0.1875 to 0.1875
- inter_qkv: bfloat16 [256, 3, 256], P(None, None, 'mp'), may hold values from -20 to 20
- inter_out: bfloat16 [256, 256], P('mp'), may hold values from -0.375 to 0.375
- inter_up: bfloat16 [256, 1024], P(None, 'mp'), may hold values from -0.375 to 0.375
- inter_down: bfloat16 [1024, 256], P('mp'), may hold values from -0.1875 to 0.1875
Outputs:
- margin_sum: bfloat16 [24000, 256], P('seq')
All inputs are finite; a program needn't handle non-finite values.
Results may differ from a plain program's by a relative error of at most 0.014.
Values may be sent and summed in bfloat16 or wider, within the bound.
A program may use at most 128 MiB of HBM per device.

v0:
```python
import jax
import jax.numpy as jnp
from jax import lax
from jax.sharding import PartitionSpec as P

HEADS = 8
HD = 32
K = 250


def passed_along(shard, axis, by):
    peers = lax.axis_size(axis)
    pairs = [(i, i + by) for i in range(peers) if 0 <= i + by < peers]
    return lax.ppermute(shard, axis, pairs)


def layer_norm(values):
    values = values.astype(jnp.float32)
    centre = values - jnp.mean(values, axis=-1, keepdims=True)
    spread = jnp.mean(centre * centre, axis=-1, keepdims=True)
    return (centre * lax.rsqrt(spread + 1e-05)).astype(jnp.bfloat16)


def attend(query_rows, key_rows, value_rows):
    factor = query_rows.shape[-1] ** (-0.5)
    scores = (
        jnp.einsum("bqhe,bkhe->bhqk", query_rows, key_rows, preferred_element_type=jnp.float32)
        * factor
    )
    scores = scores - jnp.max(scores, axis=-1, keepdims=True)
    weights = jnp.exp(scores)
    weights = (weights / jnp.sum(weights, axis=-1, keepdims=True)).astype(jnp.bfloat16)
    return jnp.einsum(
        "bhqk,bkhe->bqhe", weights, value_rows, preferred_element_type=jnp.float32
    ).astype(jnp.bfloat16)


def attend_rows(query_rows, key_rows, value_rows, per_step):
    blocks = query_rows.shape[0] // per_step
    stacked = tuple(
        (
            member.reshape((blocks, per_step) + member.shape[1:])
            for member in (query_rows, key_rows, value_rows)
        )
    )
    attended = lax.map(lambda pieces: attend(pieces[0], pieces[1], pieces[2]), stacked)
    return attended.reshape(query_rows.shape)


def whole_block(stream, qkv_weight, out_weight, up_weight, down_weight):
    normed = layer_norm(stream)
    projected = jnp.einsum(
        "pcd,dtj->tpcj", normed, qkv_weight, preferred_element_type=jnp.float32
    ).astype(jnp.bfloat16)
    projected = projected.reshape(3, stream.shape[0], stream.shape[1], HEADS, HD)
    attended = attend_rows(projected[0], projected[1], projected[2], 1)
    branch = jnp.einsum(
        "pche,hed->pcd",
        attended,
        out_weight.reshape(HEADS, HD, -1),
        preferred_element_type=jnp.float32,
    )
    middle = (stream.astype(jnp.float32) + branch).astype(jnp.bfloat16)
    normed = layer_norm(middle)
    hidden = jax.nn.relu(
        jnp.einsum("pcd,df->pcf", normed, up_weight, preferred_element_type=jnp.float32)
    ).astype(jnp.bfloat16)
    branch = jnp.einsum("pcf,fd->pcd", hidden, down_weight, preferred_element_type=jnp.float32)
    return (middle.astype(jnp.float32) + branch).astype(jnp.bfloat16)


def on_device(
    frames, intra_qkv, intra_out, intra_up, intra_down, inter_qkv, inter_out, inter_up, inter_down
):
    seq_count = lax.axis_size("seq")
    model_count = lax.axis_size("mp")
    intra_full = (
        lax.all_gather(intra_qkv, "mp", axis=2, tiled=True),
        lax.all_gather(intra_out, "mp", axis=0, tiled=True),
        lax.all_gather(intra_up, "mp", axis=1, tiled=True),
        lax.all_gather(intra_down, "mp", axis=0, tiled=True),
    )
    span_count = frames.shape[0] // model_count
    own_spans = lax.dynamic_slice_in_dim(frames, lax.axis_index("mp") * span_count, span_count, 0)
    finished = whole_block(own_spans, intra_full[0], intra_full[1], intra_full[2], intra_full[3])
    stream = lax.all_gather(finished, "mp", axis=0, tiled=True)
    spread_devices = seq_count * model_count
    padded_len = (K + spread_devices - 1) // spread_devices * spread_devices
    full_weights = (
        lax.all_gather(inter_qkv, "mp", axis=2, tiled=True),
        lax.all_gather(inter_out, "mp", axis=0, tiled=True),
        lax.all_gather(inter_up, "mp", axis=1, tiled=True),
        lax.all_gather(inter_down, "mp", axis=0, tiled=True),
    )
    per_device = padded_len // spread_devices
    arranged = jnp.pad(jnp.transpose(stream, (1, 0, 2)), ((0, padded_len - K), (0, 0), (0, 0)))
    arranged = arranged.reshape(
        seq_count, model_count, per_device, stream.shape[0], stream.shape[2]
    )
    mine = lax.dynamic_index_in_dim(arranged, lax.axis_index("mp"), 1, keepdims=False)
    mine = mine.reshape(seq_count * per_device, stream.shape[0], stream.shape[2])
    spread_rows = lax.all_to_all(mine, "seq", split_axis=0, concat_axis=1, tiled=True)
    spread_rows = whole_block(
        spread_rows, full_weights[0], full_weights[1], full_weights[2], full_weights[3]
    )
    returned = lax.all_to_all(spread_rows, "seq", split_axis=1, concat_axis=0, tiled=True)
    returned = returned.reshape(seq_count, 1, per_device, stream.shape[0], stream.shape[2])
    collected = lax.all_gather(returned, "mp", axis=1, tiled=True)
    collected = collected.reshape(padded_len, stream.shape[0], stream.shape[2])
    stream = jnp.transpose(collected[:K], (1, 0, 2))
    hop_len = K // 2
    tail_rows = stream[:, hop_len:]
    carried = passed_along(tail_rows[-1], "seq", 1)
    earlier = jnp.concatenate([carried[None], tail_rows[:-1]], axis=0)
    summed = stream[:, :hop_len].astype(jnp.float32) + earlier.astype(jnp.float32)
    return summed.astype(jnp.bfloat16).reshape(-1, stream.shape[2])


def solution(mesh):
    return jax.shard_map(
        on_device,
        mesh=mesh,
        in_specs=(
            P("seq", None, None),
            P(None, None, "mp"),
            P("mp", None),
            P(None, "mp"),
            P("mp", None),
            P(None, None, "mp"),
            P("mp", None),
            P(None, "mp"),
            P("mp", None),
        ),
        out_specs=P("seq", None),
        check_vma=False,
    )
```

profile of v0, /device:TPU:4, one launch (start us, length us, event | category | flops | bytes accessed | tf_op | source)
XLA Modules:
  0.0 418.6 jit_solution(934940214543586257)
XLA Ops:
  9.6 14.8 %all_gather.30 = bf16[256,3,256]{0,2,1:T(8,128)(2,1)S(1)} all-gather(bf16[256,3,64]{0,2,1:T(8,128)(2,1)S(1)} %copy-done.7), channel_id=1, replica_groups=mesh['seq'=8,'mp'=4] {'mp'}, dimensions={2}, use_global_device_ids=true | all-gather | bytes 491520 | tf_op jit(solution)/shard_map/all_gather | solution.py:78
  33.7 27.5 %while.20 = (s32[]{:T(128)}, bf16[6,1,250,8,32]{2,4,3,1,0:T(8,128)(2,1)}, bf16[6,1,250,8,32]{2,4,3,1,0:T(8,128)(2,1)}, bf16[6,1,250,8,32]{2,4,3,1,0:T(8,128)(2,1...) while((s32[]{:T(128)}, bf16[6,1,250,8,32]{2,4,3,1,0:T(8,128)(2,1)}, bf16[6,1,250,8,32]{2,4,3,1,0:T(8,128)(2,1)}, ...), condition=%wide.region_5.6_spmd, body=%wide.region_2.5_spmd.sunk | while | flops 99566496 | bytes 805573 | solution.py:46
  35.6 2.7 fusion.164
  40.2 2.7 fusion.164
  44.8 2.7 fusion.164
  49.3 2.8 fusion.164
  53.9 2.7 fusion.164
  58.5 2.7 fusion.164
  61.3 13.8 %all_gather.31 = bf16[256,256]{1,0:T(8,128)(2,1)S(1)} all-gather(bf16[64,256]{1,0:T(8,128)(2,1)S(1)} %copy-done.8), channel_id=1, replica_groups=mesh['seq'=8,'mp'=4] {'mp'}, dimensions={0}, use_global_device_ids=true | all-gather | bytes 163840 | tf_op jit(solution)/shard_map/all_gather | solution.py:79
  78.5 16.5 %all_gather.32 = bf16[256,1024]{1,0:T(8,128)(2,1)} all-gather(bf16[256,256]{1,0:T(8,128)(2,1)S(1)} %copy-done.4), channel_id=1, replica_groups=mesh['seq'=8,'mp'=4] {'mp'}, dimensions={1}, use_global_device_ids=true | all-gather | bytes 655360 | tf_op jit(solution)/shard_map/all_gather | solution.py:80
  95.0 15.7 %all_gather.33 = bf16[1024,256]{1,0:T(8,128)(2,1)} all-gather(bf16[256,256]{1,0:T(8,128)(2,1)S(1)} %copy-done.5), channel_id=1, replica_groups=mesh['seq'=8,'mp'=4] {'mp'}, dimensions={0}, use_global_device_ids=true | all-gather | bytes 655360 | tf_op jit(solution)/shard_map/all_gather | solution.py:81
  110.7 4.5 %fusion.94 = bf16[6,250,256]{2,1,0:T(8,128)(2,1)} fusion(bf16[6,250,256]{2,1,0:T(8,128)(2,1)} %copy-done.3, f32[6,250]{1,0:T(8,128)S(1)} %add_rsqrt_fusion.2, f32[6,250]{1,0:T(8,128)S(1)} %broadcast_multiply_fusion.2, bf16[1024,256]{1,0:T(8,128)(2,1)} %all_gather.33, bf16[256,1024]{1,0:T(8,128)(2,1)} %all_gather.32), kind=kOutput, calls=%fused_computation.84 | convolution fusion | flops 1578624000 | bytes 2596576 | tf_op jit(solution)/shard_map/pcf,fd->pcd/dot_general | solution.py:68
  115.3 65.1 %all-gather.4.cloned.1.call-done = bf16[24,250,256]{2,1,0:T(8,128)(2,1)} async-done(((bf16[6,250,256]{2,1,0:T(8,128)(2,1)}), bf16[24,250,256]{2,1,0:T(8,128)(2,1)}) %all-gather.4.cloned.1.call-update) | async-done | bytes 3072016 | tf_op jit(solution)/shard_map/all_gather | solution.py:86
  184.1 4.7 %all-to-all-start = ((bf16[64,24,256]{2,1,0:T(8,128)(2,1)}), bf16[64,24,256]{2,1,0:T(8,128)(2,1)}, u32[]{:S(2)}, u32[]{:S(2)}) async-start(bf16[64,24,256]{2,1,0:T(8,128)(2,1)} %bitcast.194), calls=%async_computation | async-start | bytes 1572864 | tf_op jit(solution)/shard_map/all_to_all | solution.py:102
  188.8 14.3 %all_gather.36 = bf16[256,256]{1,0:T(8,128)(2,1)} all-gather(bf16[64,256]{1,0:T(8,128)(2,1)S(1)} %copy-done.9), channel_id=1, replica_groups=mesh['seq'=8,'mp'=4] {'mp'}, dimensions={0}, use_global_device_ids=true | all-gather | bytes 163840 | tf_op jit(solution)/shard_map/all_gather | solution.py:91
  203.1 14.5 %all_gather.35 = bf16[256,3,256]{0,2,1:T(8,128)(2,1)S(1)} all-gather(bf16[256,3,64]{0,2,1:T(8,128)(2,1)} %param.18), channel_id=1, replica_groups=mesh['seq'=8,'mp'=4] {'mp'}, dimensions={2}, use_global_device_ids=true | all-gather | bytes 491520 | tf_op jit(solution)/shard_map/all_gather | solution.py:90
  217.6 16.9 %all_gather.37 = bf16[256,1024]{1,0:T(8,128)(2,1)} all-gather(bf16[256,256]{1,0:T(8,128)(2,1)} %param.20), channel_id=1, replica_groups=mesh['seq'=8,'mp'=4] {'mp'}, dimensions={1}, use_global_device_ids=true | all-gather | bytes 655360 | tf_op jit(solution)/shard_map/all_gather | solution.py:92
  234.5 15.8 %all_gather.38 = bf16[1024,256]{1,0:T(8,128)(2,1)} all-gather(bf16[256,256]{1,0:T(8,128)(2,1)} %param.21), channel_id=1, replica_groups=mesh['seq'=8,'mp'=4] {'mp'}, dimensions={0}, use_global_device_ids=true | all-gather | bytes 655360 | tf_op jit(solution)/shard_map/all_gather | solution.py:93
  267.2 41.7 %while.21 = (s32[]{:T(128)}, bf16[8,1,192,8,32]{2,4,3,1,0:T(8,128)(2,1)}, bf16[8,1,192,8,32]{2,4,3,1,0:T(8,128)(2,1)}, bf16[8,1,192,8,32]{2,4,3,1,0:T(8,128)(2,1...) while((s32[]{:T(128)}, bf16[8,1,192,8,32]{2,4,3,1,0:T(8,128)(2,1)}, ...), condition=%wide.region_13.14_spmd, body=%wide.region_10.13_spmd.sunk | while | flops 39272640 | bytes 3291205 | solution.py:46
  267.2 2.8 fusion.168
  272.4 2.8 fusion.168
  277.6 2.8 fusion.168
  282.9 2.8 fusion.168
  288.1 2.8 fusion.168
  293.3 2.8 fusion.168
  298.5 2.8 fusion.168
  303.7 2.8 fusion.168
  312.7 4.5 %fusion.95 = bf16[8,192,256]{2,1,0:T(8,128)(2,1)} fusion(bf16[8,192,256]{2,1,0:T(8,128)(2,1)} %copy-done.2, f32[8,192]{1,0:T(8,128)S(1)} %add_rsqrt_fusion.1, f32[8,192]{1,0:T(8,128)S(1)} %broadcast_multiply_fusion.1, bf16[1024,256]{1,0:T(8,128)(2,1)} %all_gather.38, bf16[256,1024]{1,0:T(8,128)(2,1)} %all_gather.37), kind=kOutput, calls=%fused_computation.85 | convolution fusion | flops 1616510976 | bytes 2633728 | tf_op jit(solution)/shard_map/pcf,fd->pcd/dot_general | solution.py:68
  318.8 15.1 %all_to_all.24 = bf16[8,192,256]{2,0,1:T(8,128)(2,1)S(1)} all-to-all(bf16[8,192,256]{2,0,1:T(8,128)(2,1)S(1)} %copy.150), channel_id=1, replica_groups=mesh['seq'=8,'mp'=4] {'seq'}, dimensions={1} | all-to-all | bytes 1572864 | tf_op jit(solution)/shard_map/all_to_all | solution.py:106
  334.9 62.6 %all-gather.6.cloned.1.call-done = bf16[8,32,24,256]{3,2,0,1:T(8,128)(2,1)} async-done(((bf16[8,8,24,256]{3,2,0,1:T(8,128)(2,1)}), bf16[8,32,24,256]{3,2,0,1:T(8,128)(2,1)}) %all-gather.6.cloned.1.call-update) | async-done | bytes 3145744 | tf_op jit(solution)/shard_map/all_gather | solution.py:108
  402.0 4.4 %collective-permute-done = bf16[125,256]{1,0:T(8,128)(2,1)S(1)} collective-permute-done((bf16[125,256]{1,0:T(8,128)(2,1)S(1)}, bf16[125,256]{1,0:T(8,128)(2,1)S(1)}, u32[]{:S(2)}, u32[]{:S(2)}) %collective-permute-start) | collective-permute-done | bytes 64032 | tf_op jit(solution)/shard_map/ppermute | solution.py:14
  409.1 2.7 reshape.186
  (90 shorter events, 80.0 us)
Async XLA Ops:
  6.5 1.9 copy-start
  6.5 173.9 %all-gather.4.cloned.1.call-start = ((), (), s32[]{:S(2)}) async-start(), calls=%async_computation.2 | async-start | bytes 3932160 | tf_op jit(solution)/shard_map/all_gather | solution.py:86
  8.4 1.2 copy-start.7
  8.7 16.7 %copy-start.1 = (bf16[6,250,256]{2,0,1:T(8,128)(2,1)}, bf16[6,250,256]{2,0,1:T(8,128)(2,1)S(1)}, u32[]{:S(2)}) copy-start(bf16[6,250,256]{2,0,1:T(8,128)(2,1)S(1)} %constant_dynamic-slice_fusion.1) | copy-start | bytes 2304004
  33.7 27.5 %copy-start.8 = (bf16[64,256]{1,0:T(8,128)(2,1)S(1)}, bf16[64,256]{1,0:T(8,128)(2,1)}, u32[]{:S(2)}) copy-start(bf16[64,256]{1,0:T(8,128)(2,1)} %param.15) | copy-start | bytes 98308
  75.1 3.4 copy-start.4
  77.1 0.9 copy-start.3
  77.1 17.9 %copy-start.5 = (bf16[256,256]{1,0:T(8,128)(2,1)S(1)}, bf16[256,256]{1,0:T(8,128)(2,1)}, u32[]{:S(2)}) copy-start(bf16[256,256]{1,0:T(8,128)(2,1)} %param.17) | copy-start | bytes 393220
  182.8 6.0 %copy-start.9 = (bf16[64,256]{1,0:T(8,128)(2,1)S(1)}, bf16[64,256]{1,0:T(8,128)(2,1)}, u32[]{:S(2)}) copy-start(bf16[64,256]{1,0:T(8,128)(2,1)} %param.19) | copy-start | bytes 98308
  184.1 66.2 %all-to-all-start = ((bf16[64,24,256]{2,1,0:T(8,128)(2,1)}), bf16[64,24,256]{2,1,0:T(8,128)(2,1)}, u32[]{:S(2)}, u32[]{:S(2)}) async-start(bf16[64,24,256]{2,1,0:T(8,128)(2,1)} %bitcast.194), calls=%async_computation | async-start | bytes 1572864 | tf_op jit(solution)/shard_map/all_to_all | solution.py:102
  188.8 208.7 %all-gather.6.cloned.1.call-start = ((), (), s32[]{:S(2)}) async-start(), calls=%async_computation.3 | async-start | bytes 3932160 | tf_op jit(solution)/shard_map/all_gather | solution.py:108
  267.2 41.7 %copy-start.6 = (bf16[256,256]{1,0:T(8,128)(2,1)S(1)}, bf16[256,256]{1,0:T(8,128)(2,1)}, u32[]{:S(2)}) copy-start(bf16[256,256]{1,0:T(8,128)(2,1)} %all_gather.36) | copy-start | bytes 393220
  311.2 0.9 copy-start.2
  399.9 6.5 %collective-permute-start = (bf16[125,256]{1,0:T(8,128)(2,1)S(1)}, bf16[125,256]{1,0:T(8,128)(2,1)S(1)}, u32[]{:S(2)}, u32[]{:S(2)}) collective-permute-start(bf16[125,256]{1,0:T(8,128)(2,1)S(1)} %bitcast.204), channel_id=1, source_target_pairs={{0,4},{4,8},{8,12},{12,16},{16,20},{20,24},{24,28},{1,5},{5,9},{9,... | collective-permute-start | bytes 192008 | tf_op jit(solution)/shard_map/ppermute | solution.py:14
Sparse Core Ops, SparseCore 0:
  115.4 64.9 all-gather.3
  335.0 62.4 all-gather.5
where the time goes:
time: 420 us; the launch traced here: 419 us
  blocking collectives  137 us (33%)
  waiting for transfers between devices  132 us (31%)
  matrix products  84.4 us (20%)
  local copies, waits for them, and re-layouts  34.7 us (8%)
  between operations  13.7 us (3%)
  other arithmetic  9.62 us (2%)
  starting transfers between devices  6.58 us (2%)
    all_gather x1, waiting for transfers between devices, on_device(): stream = lax.all_gather(finished, 'mp', axis=0, tiled=True)  65.1 us
    all_gather x1, waiting for transfers between devices, on_device(): collected = lax.all_gather(returned, 'mp', axis=1, tiled=True)  62.6 us
    dot_general x14, matrix products, attend(): jnp.einsum('bhqk,bkhe->bqhe', weights, value_rows, preferred_element_type...  35.7 us
    sub x14, matrix products, attend(): scores = scores - jnp.max(scores, axis=-1, keepdims=True)  33.5 us
    all_gather x1, blocking collectives, on_device(): lax.all_gather(inter_up, 'mp', axis=1, tiled=True)  16.9 us
    slice x8, local copies, waits for them, and re-layouts, whole_block(): attended = attend_rows(projected[0], projected[1], projected[2], 1)  16.6 us
    all_gather x1, blocking collectives, on_device(): lax.all_gather(intra_up, 'mp', axis=1, tiled=True)  16.5 us
    all_gather x1, blocking collectives, on_device(): lax.all_gather(inter_down, 'mp', axis=0, tiled=True)  15.8 us
  transfers between devices with their start and end apart: 4, of which 3 were waited for; matrix products, arithmetic and copies ran while one was open for 0% of the time, Pallas kernels for 0%

commit v1 on v0

--- a/solution.py
+++ b/solution.py
@@ -105,7 +105,13 @@
     )
     returned = lax.all_to_all(spread_rows, "seq", split_axis=1, concat_axis=0, tiled=True)
     returned = returned.reshape(seq_count, 1, per_device, stream.shape[0], stream.shape[2])
-    collected = lax.all_gather(returned, "mp", axis=1, tiled=True)
+    size = lax.axis_size("mp")
+    moving, tiles = (returned, [returned])
+    for _ in range(size - 1):
+        moving = lax.ppermute(moving, "mp", [(i_2, (i_2 + 1) % size) for i_2 in range(size)])
+        tiles.insert(0, moving)
+    merged = jnp.concatenate(tiles, axis=1)
+    collected = jnp.roll(merged, (lax.axis_index("mp") + 1) * returned.shape[1], axis=1)
     collected = collected.reshape(padded_len, stream.shape[0], stream.shape[2])
     stream = jnp.transpose(collected[:K], (1, 0, 2))
     hop_len = K // 2

time: 420 us -> 396 us (0.943)
  local copies, waits for them, and re-layouts: 34.7 us -> 22.8 us
  waiting for transfers between devices: 132 us -> 127 us
  other arithmetic: 9.62 us -> 4.79 us
  matrix products: 84.4 us -> 79.9 us
    all_gather x1 -> x0, waiting for transfers between devices: 62.6 us -> none  [on_device(): collected = lax.all_gather(returned, 'mp', axis=1, tiled=True)]
    ppermute x0 -> x3, waiting for transfers between devices: none -> 58.7 us  [on_device(): lax.ppermute(moving, 'mp', [(i_2, (i_2 + 1) % size) for i_2 in range(size)])]
    slice x8, local copies, waits for them, and re-layouts: 16.6 us -> 9.81 us  [whole_block(): attended = attend_rows(projected[0], projected[1], projected[2], 1)]
  transfers between devices with their start and end apart: 4 -> 6, of which waited for: 3 -> 5; matrix products, arithmetic and copies ran while one was open for 0% -> 0% of each run, Pallas kernels for 0% -> 0%
where the time goes in v1:
time: 396 us; the launch traced here: 393 us
  blocking collectives  139 us (35%)
  waiting for transfers between devices  127 us (32%)
  matrix products  79.9 us (20%)
  local copies, waits for them, and re-layouts  22.8 us (6%)
  between operations  13.8 us (3%)
  starting transfers between devices  6.59 us (2%)
  other arithmetic  4.79 us (1%)
    all_gather x1, waiting for transfers between devices, on_device(): stream = lax.all_gather(finished, 'mp', axis=0, tiled=True)  63.6 us
    ppermute x3, waiting for transfers between devices, on_device(): lax.ppermute(moving, 'mp', [(i_2, (i_2 + 1) % size) for i_2 in range(size)])  58.7 us
    dot_general x14, matrix products, attend(): jnp.einsum('bhqk,bkhe->bqhe', weights, value_rows, preferred_element_type...  35.4 us
    sub x14, matrix products, attend(): scores = scores - jnp.max(scores, axis=-1, keepdims=True)  33.3 us
    all_gather x1, blocking collectives, on_device(): lax.all_gather(intra_up, 'mp', axis=1, tiled=True)  17.2 us
    all_gather x1, blocking collectives, on_device(): lax.all_gather(inter_up, 'mp', axis=1, tiled=True)  16.5 us
    all_gather x1, blocking collectives, on_device(): lax.all_gather(intra_down, 'mp', axis=0, tiled=True)  15.8 us
    all_gather x1, blocking collectives, on_device(): lax.all_gather(intra_out, 'mp', axis=0, tiled=True)  15.7 us
  transfers between devices with their start and end apart: 6, of which 5 were waited for; matrix products, arithmetic and copies ran while one was open for 0% of the time, Pallas kernels for 0%

profile of v1, /device:TPU:4, one launch (start us, length us, event | category | flops | bytes accessed | tf_op | source)
XLA Modules:
  0.0 393.5 jit_solution(9650580714763573197)
XLA Ops:
  6.5 15.7 %all_gather.28 = bf16[256,256]{1,0:T(8,128)(2,1)} all-gather(bf16[64,256]{1,0:T(8,128)(2,1)} %param.15), channel_id=1, replica_groups=mesh['seq'=8,'mp'=4] {'mp'}, dimensions={0}, use_global_device_ids=true | all-gather | bytes 163840 | tf_op jit(solution)/shard_map/all_gather | solution.py:79
  22.3 14.8 %all_gather.27 = bf16[256,3,256]{0,2,1:T(8,128)(2,1)S(1)} all-gather(bf16[256,3,64]{0,2,1:T(8,128)(2,1)} %param.14), channel_id=1, replica_groups=mesh['seq'=8,'mp'=4] {'mp'}, dimensions={2}, use_global_device_ids=true | all-gather | bytes 491520 | tf_op jit(solution)/shard_map/all_gather | solution.py:78
  37.1 17.2 %all_gather.29 = bf16[256,1024]{1,0:T(8,128)(2,1)} all-gather(bf16[256,256]{1,0:T(8,128)(2,1)} %param.16), channel_id=1, replica_groups=mesh['seq'=8,'mp'=4] {'mp'}, dimensions={1}, use_global_device_ids=true | all-gather | bytes 655360 | tf_op jit(solution)/shard_map/all_gather | solution.py:80
  54.4 15.8 %all_gather.30 = bf16[1024,256]{1,0:T(8,128)(2,1)} all-gather(bf16[256,256]{1,0:T(8,128)(2,1)} %param.17), channel_id=1, replica_groups=mesh['seq'=8,'mp'=4] {'mp'}, dimensions={0}, use_global_device_ids=true | all-gather | bytes 655360 | tf_op jit(solution)/shard_map/all_gather | solution.py:81
  75.1 26.9 %while.20 = (s32[]{:T(128)}, bf16[6,1,250,8,32]{2,4,3,1,0:T(8,128)(2,1)}, bf16[6,1,250,8,32]{2,4,3,1,0:T(8,128)(2,1)}, bf16[6,1,250,8,32]{2,4,3,1,0:T(8,128)(2,1...) while((s32[]{:T(128)}, bf16[6,1,250,8,32]{2,4,3,1,0:T(8,128)(2,1)}, ...), condition=%wide.region_5.6_spmd, body=%wide.region_2.5_spmd.sunk | while | flops 99566496 | bytes 805773 | solution.py:46
  77.0 2.7 fusion.164
  81.5 2.7 fusion.164
  90.4 2.7 fusion.164
  94.9 2.7 fusion.164
  99.4 2.7 fusion.164
  104.4 2.8 fusion.94
  107.3 63.6 %all-gather.2.cloned.1.call-done = bf16[24,250,256]{2,1,0:T(8,128)(2,1)} async-done(((bf16[6,250,256]{2,1,0:T(8,128)(2,1)}), bf16[24,250,256]{2,1,0:T(8,128)(2,1)}) %all-gather.2.cloned.1.call-update) | async-done | bytes 3072016 | tf_op jit(solution)/shard_map/all_gather | solution.py:86
  174.5 4.2 %all-to-all-start = ((bf16[64,24,256]{2,1,0:T(8,128)(2,1)}), bf16[64,24,256]{2,1,0:T(8,128)(2,1)S(1)}, u32[]{:S(2)}, u32[]{:S(2)}) async-start(bf16[64,24,256]{2,1,0:T(8,128)(2,1)} %bitcast.31), calls=%async_computation | async-start | bytes 1572864 | tf_op jit(solution)/shard_map/all_to_all | solution.py:102
  178.7 13.7 %all_gather.33 = bf16[256,256]{1,0:T(8,128)(2,1)S(1)} all-gather(bf16[64,256]{1,0:T(8,128)(2,1)S(1)} %copy-done.11), channel_id=1, replica_groups=mesh['seq'=8,'mp'=4] {'mp'}, dimensions={0}, use_global_device_ids=true | all-gather | bytes 163840 | tf_op jit(solution)/shard_map/all_gather | solution.py:91
  192.4 14.3 %all_gather.32 = bf16[256,3,256]{0,2,1:T(8,128)(2,1)S(1)} all-gather(bf16[256,3,64]{0,2,1:T(8,128)(2,1)S(1)} %copy-done.10), channel_id=1, replica_groups=mesh['seq'=8,'mp'=4] {'mp'}, dimensions={2}, use_global_device_ids=true | all-gather | bytes 491520 | tf_op jit(solution)/shard_map/all_gather | solution.py:90
  206.7 16.5 %all_gather.34 = bf16[256,1024]{1,0:T(8,128)(2,1)} all-gather(bf16[256,256]{1,0:T(8,128)(2,1)S(1)} %copy-done.7), channel_id=1, replica_groups=mesh['seq'=8,'mp'=4] {'mp'}, dimensions={1}, use_global_device_ids=true | all-gather | bytes 655360 | tf_op jit(solution)/shard_map/all_gather | solution.py:92
  223.2 15.6 %all_gather.35 = bf16[1024,256]{1,0:T(8,128)(2,1)} all-gather(bf16[256,256]{1,0:T(8,128)(2,1)S(1)} %copy-done.8), channel_id=1, replica_groups=mesh['seq'=8,'mp'=4] {'mp'}, dimensions={0}, use_global_device_ids=true | all-gather | bytes 655360 | tf_op jit(solution)/shard_map/all_gather | solution.py:93
  248.5 41.8 %while.21 = (s32[]{:T(128)}, bf16[8,1,192,8,32]{2,4,3,1,0:T(8,128)(2,1)}, bf16[8,1,192,8,32]{2,4,3,1,0:T(8,128)(2,1)}, bf16[8,1,192,8,32]{2,4,3,1,0:T(8,128)(2,1...) while((s32[]{:T(128)}, bf16[8,1,192,8,32]{2,4,3,1,0:T(8,128)(2,1)}, ...), condition=%wide.region_13.14_spmd, body=%wide.region_10.13_spmd.sunk | while | flops 39272640 | bytes 3291213 | solution.py:46
  248.5 2.8 fusion.168
  253.8 2.8 fusion.168
  259.0 2.8 fusion.168
  264.2 2.8 fusion.168
  269.4 2.8 fusion.168
  274.7 2.8 fusion.168
  279.9 2.8 fusion.168
  285.1 2.8 fusion.168
  293.1 3.0 fusion.95
  296.5 15.1 %all_to_all.24 = bf16[8,192,256]{2,0,1:T(8,128)(2,1)S(1)} all-to-all(bf16[8,192,256]{2,0,1:T(8,128)(2,1)S(1)} %copy.126), channel_id=1, replica_groups=mesh['seq'=8,'mp'=4] {'seq'}, dimensions={1} | all-to-all | bytes 1572864 | tf_op jit(solution)/shard_map/all_to_all | solution.py:106
  312.2 20.1 %collective-permute-done = bf16[8,1,8,24,256]{4,3,0,2,1:T(8,128)(2,1)S(1)} collective-permute-done((bf16[8,1,8,24,256]{4,3,0,2,1:T(8,128)(2,1)S(1)}, bf16[8,1,8,24,256]{4,3,0,2,1:T(8,128)(2,1)S(1)}, u32[]{:S(2)}, u32[]{:S(2)}) %collective-permute-start) | collective-permute-done | bytes 786464 | tf_op jit(solution)/shard_map/ppermute | solution.py:111
  332.3 19.7 %collective-permute-done.1 = bf16[8,1,8,24,256]{4,3,0,2,1:T(8,128)(2,1)S(1)} collective-permute-done((bf16[8,1,8,24,256]{4,3,0,2,1:T(8,128)(2,1)S(1)}, bf16[8,1,8,24,256]{4,3,0,2,1:T(8,128)(2,1)S(1)}, u32[]{:S(2)}, u32[]{:S(2)}) %collective-permute-start.1) | collective-permute-done | bytes 786464 | tf_op jit(solution)/shard_map/ppermute | solution.py:111
  352.0 18.9 %collective-permute-done.2 = bf16[8,1,8,24,256]{4,3,0,2,1:T(8,128)(2,1)} collective-permute-done((bf16[8,1,8,24,256]{4,3,0,2,1:T(8,128)(2,1)S(1)}, bf16[8,1,8,24,256]{4,3,0,2,1:T(8,128)(2,1)}, u32[]{:S(2)}, u32[]{:S(2)}) %collective-permute-start.2) | collective-permute-done | bytes 786464 | tf_op jit(solution)/shard_map/ppermute | solution.py:111
  376.8 4.4 %collective-permute-done.3 = bf16[125,256]{1,0:T(8,128)(2,1)S(1)} collective-permute-done((bf16[125,256]{1,0:T(8,128)(2,1)S(1)}, bf16[125,256]{1,0:T(8,128)(2,1)S(1)}, u32[]{:S(2)}, u32[]{:S(2)}) %collective-permute-start.3) | collective-permute-done | bytes 64032 | tf_op jit(solution)/shard_map/ppermute | solution.py:14
  (106 shorter events, 68.1 us)
Async XLA Ops:
  6.5 63.6 %copy-start = (bf16[24,250,256]{2,0,1:T(8,128)(2,1)S(1)}, bf16[24,250,256]{2,0,1:T(8,128)(2,1)}, u32[]{:S(2)}) copy-start(bf16[24,250,256]{2,0,1:T(8,128)(2,1)} %param.13) | copy-start | bytes 9216004
  6.5 164.3 %all-gather.2.cloned.1.call-start = ((), (), s32[]{:S(2)}) async-start(), calls=%async_computation.2 | async-start | bytes 3932160 | tf_op jit(solution)/shard_map/all_gather | solution.py:86
  70.5 1.9 copy-start.2
  75.1 27.0 %copy-start.3 = (bf16[6,250,256]{2,0,1:T(8,128)(2,1)S(1)}, bf16[6,250,256]{2,0,1:T(8,128)(2,1)}, u32[]{:S(2)}) copy-start(bf16[6,250,256]{2,0,1:T(8,128)(2,1)} %copy-done.2) | copy-start | bytes 2304004
  75.1 27.0 %copy-start.9 = (bf16[256,256]{1,0:T(8,128)(2,1)S(1)}, bf16[256,256]{1,0:T(8,128)(2,1)}, u32[]{:S(2)}) copy-start(bf16[256,256]{1,0:T(8,128)(2,1)} %all_gather.28) | copy-start | bytes 393220
  102.1 2.3 copy-start.5
  102.1 2.3 copy-start.6
  173.1 5.7 %copy-start.11 = (bf16[64,256]{1,0:T(8,128)(2,1)S(1)}, bf16[64,256]{1,0:T(8,128)(2,1)}, u32[]{:S(2)}) copy-start(bf16[64,256]{1,0:T(8,128)(2,1)} %param.19) | copy-start | bytes 98308
  173.1 19.3 %copy-start.10 = (bf16[256,3,64]{0,2,1:T(8,128)(2,1)S(1)}, bf16[256,3,64]{0,2,1:T(8,128)(2,1)}, u32[]{:S(2)}) copy-start(bf16[256,3,64]{0,2,1:T(8,128)(2,1)} %param.18) | copy-start | bytes 294916
  173.2 33.5 %copy-start.7 = (bf16[256,256]{1,0:T(8,128)(2,1)S(1)}, bf16[256,256]{1,0:T(8,128)(2,1)}, u32[]{:S(2)}) copy-start(bf16[256,256]{1,0:T(8,128)(2,1)} %param.20) | copy-start | bytes 393220
  173.2 50.0 %copy-start.8 = (bf16[256,256]{1,0:T(8,128)(2,1)S(1)}, bf16[256,256]{1,0:T(8,128)(2,1)}, u32[]{:S(2)}) copy-start(bf16[256,256]{1,0:T(8,128)(2,1)} %param.21) | copy-start | bytes 393220
  174.5 64.3 %all-to-all-start = ((bf16[64,24,256]{2,1,0:T(8,128)(2,1)}), bf16[64,24,256]{2,1,0:T(8,128)(2,1)S(1)}, u32[]{:S(2)}, u32[]{:S(2)}) async-start(bf16[64,24,256]{2,1,0:T(8,128)(2,1)} %bitcast.31), calls=%async_computation | async-start | bytes 1572864 | tf_op jit(solution)/shard_map/all_to_all | solution.py:102
  290.3 2.8 copy-start.4
  311.8 20.6 %collective-permute-start = (bf16[8,1,8,24,256]{4,3,0,2,1:T(8,128)(2,1)S(1)}, bf16[8,1,8,24,256]{4,3,0,2,1:T(8,128)(2,1)S(1)}, u32[]{:S(2)}, u32[]{:S(2)}) collective-permute-start(bf16[8,1,8,24,256]{4,3,0,2,1:T(8,128)(2,1)S(1)} %bitcast.196), channel_id=1, source_target_pairs={{0,1},{1,2},{2,3},{3,0},{4,5},{5,6},{6,7},{7,4},{8,9},{9,10},{10,1... | collective-permute-start | bytes 2359304 | tf_op jit(solution)/shard_map/ppermute | solution.py:111
  332.3 19.7 %collective-permute-start.1 = (bf16[8,1,8,24,256]{4,3,0,2,1:T(8,128)(2,1)S(1)}, bf16[8,1,8,24,256]{4,3,0,2,1:T(8,128)(2,1)S(1)}, u32[]{:S(2)}, u32[]{:S(2)}) collective-permute-start(bf16[8,1,8,24,256]{4,3,0,2,1:T(8,128)(2,1)S(1)} %collective-permute-done), channel_id=1, source_target_pairs={{0,1},{1,2},{2,3},{3,0},{4,5},{5,6},{6,7},{7,4},{8,9},{9,10},{10,1... | collective-permute-start | bytes 2359304 | tf_op jit(solution)/shard_map/ppermute | solution.py:111
  352.0 18.9 %collective-permute-start.2 = (bf16[8,1,8,24,256]{4,3,0,2,1:T(8,128)(2,1)S(1)}, bf16[8,1,8,24,256]{4,3,0,2,1:T(8,128)(2,1)}, u32[]{:S(2)}, u32[]{:S(2)}) collective-permute-start(bf16[8,1,8,24,256]{4,3,0,2,1:T(8,128)(2,1)S(1)} %collective-permute-done.1), channel_id=1, source_target_pairs={{0,1},{1,2},{2,3},{3,0},{4,5},{5,6},{6,7},{7,4},{8,9},{9,10},{10,1... | collective-permute-start | bytes 2359304 | tf_op jit(solution)/shard_map/ppermute | solution.py:111
  374.8 6.5 %collective-permute-start.3 = (bf16[125,256]{1,0:T(8,128)(2,1)S(1)}, bf16[125,256]{1,0:T(8,128)(2,1)S(1)}, u32[]{:S(2)}, u32[]{:S(2)}) collective-permute-start(bf16[125,256]{1,0:T(8,128)(2,1)S(1)} %bitcast.209), channel_id=1, source_target_pairs={{0,4},{4,8},{8,12},{12,16},{16,20},{20,24},{24,28},{1,5},{5,9},{9,... | collective-permute-start | bytes 192008 | tf_op jit(solution)/shard_map/ppermute | solution.py:14
  382.4 4.2 %copy-start.1 = (bf16[24,250,256]{2,0,1:T(8,128)(2,1)S(1)}, bf16[24,250,256]{2,0,1:T(8,128)(2,1)}, u32[]{:S(2)}) copy-start(bf16[24,250,256]{2,0,1:T(8,128)(2,1)} %param.13) | copy-start | bytes 9216004
Sparse Core Ops, SparseCore 0:
  107.4 63.4 all-gather.1
